TPU v7x, 8 devices: a whole 2x2x1 slice. The times are simulated.
8 devices in a mesh: g: 1 (over z), y: 2 (over y), x: 4 (over x, core).
Axes of the slice: x: 2, y: 2, z: 1, core: 2. Of those that a mesh axis runs over, the one named last changes fastest.
Arguments:
- source: float32 [96, 96, 200], P(('g', 'x'), 'y')
- sigma_t: float32 [96, 96, 200], P(('g', 'x'), 'y')
- cos_x: float32 [10], replicated
- cos_y: float32 [10], replicated
- cos_z: float32 [10], replicated
- weights: float32 [10], replicated
Outputs:
- output: float32 [96, 96, 200], P(('g', 'x'), 'y')
All inputs are finite; a program needn't handle non-finite values.
Results may differ from a plain program's by a relative error of at most 0.001.
Values sent between devices are 32-bit elements.
A program may use at most 1 GiB of HBM per device.

v0:
```python
import jax
import jax.numpy as jnp
from jax import lax
from jax.sharding import PartitionSpec as P


def skew_last(values):
    n_rows, n_cols = values.shape[-2], values.shape[-1]
    lead_dims = values.shape[:-2]
    widths = [(0, 0)] * len(lead_dims) + [(0, 0), (0, n_rows)]
    flat_vals = jnp.pad(values, widths).reshape(lead_dims + (n_rows * (n_cols + n_rows),))
    kept_vals = flat_vals[..., : n_rows * (n_cols + n_rows - 1)]
    return kept_vals.reshape(lead_dims + (n_rows, n_cols + n_rows - 1))


def unskew_last(values, length):
    n_rows, n_cols = values.shape[-2], values.shape[-1]
    lead_dims = values.shape[:-2]
    flat_vals = values.reshape(lead_dims + (n_rows * n_cols,))
    flat_vals = jnp.pad(flat_vals, [(0, 0)] * len(lead_dims) + [(0, n_rows)])
    return flat_vals.reshape(lead_dims + (n_rows, n_cols + 1))[..., :length]


def skew_grid(grid_arr):
    first_pass = skew_last(grid_arr)
    second_pass = skew_last(jnp.transpose(first_pass, (0, 2, 1, 3)))
    return jnp.transpose(second_pass, (3, 0, 2, 1))


def unskew_grid(skewed, size_z):
    size_y = skewed.shape[3]
    first_pass = unskew_last(jnp.transpose(skewed, (1, 3, 2, 0)), size_z + size_y - 1)
    return unskew_last(jnp.transpose(first_pass, (0, 2, 1, 3)), size_z)


def face_to_skew(face_arr, n_steps):
    size_n, size_l = face_arr.shape[1], face_arr.shape[2]
    skewed = skew_last(jnp.transpose(face_arr, (0, 3, 1, 2)))
    skewed = jnp.pad(skewed, ((0, 0), (0, 0), (0, 0), (0, n_steps - size_l - size_n + 1)))
    return jnp.transpose(skewed, (3, 0, 2, 1))


def skew_to_face(skewed, offset, size_l):
    tail_part = jnp.transpose(skewed[offset:], (1, 3, 2, 0))
    return jnp.transpose(unskew_last(tail_part, size_l), (0, 2, 3, 1))


def sweep_box(src_sk, sig_sk, xin_sk, yin_sk, z_in, cos_x, cos_y, cos_z, weights, size_l):
    n_steps, size_x, size_y = src_sk.shape[0], src_sk.shape[2], src_sk.shape[3]
    coef_x = 2.0 * cos_x
    coef_y = 2.0 * cos_y
    coef_z = 2.0 * cos_z
    coef_sum = coef_x + coef_y + coef_z
    diagonal = jnp.arange(size_x)[:, None] + jnp.arange(size_y)[None, :]

    def plane_step(carry_in, inputs):
        face_x, face_y, face_z = carry_in
        src_t, sig_t, edge_x, edge_y, step_idx = inputs
        in_x = jnp.concatenate([edge_x[:, None], face_x[:, :-1]], axis=1)
        in_y = jnp.concatenate([edge_y[:, :, None], face_y[:, :, :-1]], axis=2)
        ang_flux = (src_t[..., None] + coef_x * in_x + coef_y * in_y + coef_z * face_z) / (sig_t[..., None] + coef_sum)
        z_level = step_idx - diagonal
        inside = ((z_level >= 0) & (z_level < size_l))[None, :, :, None]
        out_x = jnp.where(inside, 2.0 * ang_flux - in_x, 0.0)
        out_y = jnp.where(inside, 2.0 * ang_flux - in_y, 0.0)
        out_z = jnp.where(inside, 2.0 * ang_flux - face_z, face_z)
        flux_t = jnp.where(inside[..., 0], jnp.sum(ang_flux * weights, axis=-1), 0.0)
        return (out_x, out_y, out_z), (flux_t, out_x[:, size_x - 1], out_y[:, :, size_y - 1])

    zero_faces = jnp.zeros_like(z_in)
    carry_out, outputs = lax.scan(plane_step, (zero_faces, zero_faces, z_in), (src_sk, sig_sk, xin_sk, yin_sk, jnp.arange(n_steps)))
    return outputs[0], outputs[1], outputs[2], carry_out[2]


def solution(mesh):
    count_x = mesh.shape["x"]
    count_y = mesh.shape["y"]
    grid_spec = P(("g", "x"), "y", None)

    def column_sweep(source, sigma_t, cos_x, cos_y, cos_z, weights):
        size_x, size_y, size_z = source.shape
        n_dirs = cos_x.shape[0]
        n_blocks = 2
        size_l = size_z // n_blocks
        n_steps = size_x + size_y + size_l - 2
        n_stages = n_blocks + count_x + count_y - 2
        rank_x = lax.axis_index("x")
        rank_y = lax.axis_index("y")
        src_two = jnp.stack([source, jnp.flip(source, 2)])
        sig_two = jnp.stack([sigma_t, jnp.flip(sigma_t, 2)])
        none_x = jnp.zeros((n_blocks, 2, size_y, size_l, n_dirs), jnp.float32)
        none_y = jnp.zeros((n_blocks, 2, size_x, size_l, n_dirs), jnp.float32)

        def corner(sign_x, sign_y, bound_x, bound_y, keep_x, keep_y):
            flip_axes = ((1,) if sign_x < 0 else ()) + ((2,) if sign_y < 0 else ())
            src_sk = skew_grid(jnp.flip(src_two, flip_axes) if flip_axes else src_two)
            sig_sk = skew_grid(jnp.flip(sig_two, flip_axes) if flip_axes else sig_two)
            up_x = rank_x if sign_x > 0 else count_x - 1 - rank_x
            up_y = rank_y if sign_y > 0 else count_y - 1 - rank_y
            perm_x = [(i, i + 1) for i in range(count_x - 1)] if sign_x > 0 else [(i + 1, i) for i in range(count_x - 1)]
            perm_y = [(i, i + 1) for i in range(count_y - 1)] if sign_y > 0 else [(i + 1, i) for i in range(count_y - 1)]

            def run_block(block_c, in_x, in_y, in_z):
                first_t = block_c * size_l
                flux_sk, xout_sk, yout_sk, out_z = sweep_box(
                    lax.dynamic_slice_in_dim(src_sk, first_t, n_steps, 0),
                    lax.dynamic_slice_in_dim(sig_sk, first_t, n_steps, 0),
                    face_to_skew(in_x, n_steps), face_to_skew(in_y, n_steps), in_z,
                    cos_x, cos_y, cos_z, weights, size_l)
                return (flux_sk, skew_to_face(xout_sk, size_x - 1, size_l), skew_to_face(yout_sk, size_y - 1, size_l), out_z)

            def skip_block(block_c, in_x, in_y, in_z):
                return (jnp.zeros((n_steps, 2, size_x, size_y), jnp.float32), jnp.zeros_like(in_x), jnp.zeros_like(in_y), in_z)

            def stage_step(stage_idx, carry_in):
                recv_x, recv_y, face_z, flux_sk, kept_x, kept_y = carry_in
                block_idx = stage_idx - up_x - up_y
                active = (block_idx >= 0) & (block_idx < n_blocks)
                block_c = jnp.clip(block_idx, 0, n_blocks - 1)
                in_x = jnp.where(up_x == 0, lax.dynamic_index_in_dim(bound_x, block_c, 0, keepdims=False), recv_x)
                in_y = jnp.where(up_y == 0, lax.dynamic_index_in_dim(bound_y, block_c, 0, keepdims=False), recv_y)
                flux_blk, out_x, out_y, face_z = lax.cond(active, run_block, skip_block, block_c, in_x, in_y, face_z)
                first_t = block_c * size_l
                window = lax.dynamic_slice_in_dim(flux_sk, first_t, n_steps, 0)
                flux_sk = lax.dynamic_update_slice_in_dim(flux_sk, window + flux_blk, first_t, 0)
                if keep_x:
                    kept_x = jnp.where(active, lax.dynamic_update_index_in_dim(kept_x, out_x, block_c, 0), kept_x)
                if keep_y:
                    kept_y = jnp.where(active, lax.dynamic_update_index_in_dim(kept_y, out_y, block_c, 0), kept_y)
                recv_x = lax.ppermute(out_x, "x", perm_x) if count_x > 1 else jnp.zeros_like(out_x)
                recv_y = lax.ppermute(out_y, "y", perm_y) if count_y > 1 else jnp.zeros_like(out_y)
                return (recv_x, recv_y, face_z, flux_sk, kept_x, kept_y)

            carry_init = (none_x[0], none_y[0], jnp.zeros((2, size_x, size_y, n_dirs), jnp.float32),
                          jnp.zeros((size_x + size_y + size_z - 2, 2, size_x, size_y), jnp.float32),
                          none_x if keep_x else None, none_y if keep_y else None)
            carry_out = lax.fori_loop(0, n_stages, stage_step, carry_init)
            corner_flux = unskew_grid(carry_out[3], size_z)
            if flip_axes:
                corner_flux = jnp.flip(corner_flux, flip_axes)
            return corner_flux, carry_out[4], carry_out[5]

        flux_mm, kept_xmm, kept_ymm = corner(-1, -1, none_x, none_y, True, True)
        flux_pm, _, kept_ypm = corner(1, -1, kept_xmm, none_y, False, True)
        flux_mp, kept_xmp, _ = corner(-1, 1, none_x, kept_ymm, True, False)
        flux_pp, _, _ = corner(1, 1, kept_xmp, kept_ypm, False, False)
        total_flux = flux_mm + flux_pm + flux_mp + flux_pp
        return total_flux[0] + jnp.flip(total_flux[1], 2)

    return jax.shard_map(column_sweep, mesh=mesh, in_specs=(grid_spec, grid_spec, P(), P(), P(), P()), out_specs=grid_spec, check_vma=False)
```

profile of v0, /device:TPU:2, one launch (start us, length us, event | category | flops | bytes accessed | tf_op | source)
XLA Modules:
  0.0 27539.4 jit_solution(17646446804113456000)
XLA Ops:
  69.9 6024.0 %while.226 = (s32[]{:T(128)}, f32[2,48,100,10]{2,1,0,3:T(8,128)}, f32[2,24,100,10]{2,1,0,3:T(8,128)S(1)}, f32[2,24,48,10]{2,1,3,0:T(8,128)S(1)}, f32[270,2,24,48...) while((s32[]{:T(128)}, f32[2,48,100,10]{2,1,0,3:T(8,128)}, ...), condition=%wide.region_6.7_spmd, body=%wide.region_0.6_spmd.sunk | while | flops 1213991 | bytes 50178208 | solution.py:137
  100.1 2366.0 %collective-permute-done.7 = f32[2,24,100,10]{2,1,0,3:T(8,128)S(1)} collective-permute-done((f32[2,24,100,10]{2,1,0,3:T(8,128)}, f32[2,24,100,10]{2,1,0,3:T(8,128)S(1)}, u32[]{:S(2)}, u32[]{:S(2)}) %collective-permute-start.7) | collective-permute-done | bytes 192032 | tf_op jit(solution)/shard_map/while/body/eval_jaxpr/ppermute | solution.py:131
  2466.2 1193.0 %conditional.8 = (f32[170,2,24,48]{3,2,1,0:T(8,128)}, f32[2,48,100,10]{2,1,0,3:T(8,128)}, f32[2,24,100,10]{2,1,0,3:T(8,128)}, f32[2,24,48,10]{2,1,3,0:T(8,128)S(...) conditional(s32[]{:T(128)} %convert_element_type.94, ...), branch_computations={%region_1.1_spmd, %region_2.5_spmd} | conditional | flops 678297 | bytes 27037300 | solution.py:122
  2466.2 7.3 constant_dynamic-slice_fusion
  2481.8 1167.3 %while.222 = (s32[]{:T(128)}, f32[2,24,48,10]{2,1,3,0:T(8,128)S(1)}, f32[2,24,48,10]{2,1,3,0:T(8,128)S(1)}, f32[2,24,48,10]{2,1,3,0:T(8,128)S(1)}, f32[170,2,24,...) while((s32[]{:T(128)}, f32[2,24,48,10]{2,1,3,0:T(8,128)S(1)}, ...), condition=%wide.region_5.4_spmd.clone, body=%wide.region_3.3_spmd.clone.sunk | while | flops 534243 | bytes 1530784 | solution.py:71
  3670.5 1193.0 %conditional.8 = (f32[170,2,24,48]{3,2,1,0:T(8,128)}, f32[2,48,100,10]{2,1,0,3:T(8,128)}, f32[2,24,100,10]{2,1,0,3:T(8,128)}, f32[2,24,48,10]{2,1,3,0:T(8,128)S(...) conditional(s32[]{:T(128)} %convert_element_type.94, ...), branch_computations={%region_1.1_spmd, %region_2.5_spmd} | conditional | flops 678297 | bytes 27037300 | solution.py:122
  3670.5 7.3 constant_dynamic-slice_fusion
  3686.1 1167.3 %while.222 = (s32[]{:T(128)}, f32[2,24,48,10]{2,1,3,0:T(8,128)S(1)}, f32[2,24,48,10]{2,1,3,0:T(8,128)S(1)}, f32[2,24,48,10]{2,1,3,0:T(8,128)S(1)}, f32[170,2,24,...) while((s32[]{:T(128)}, f32[2,24,48,10]{2,1,3,0:T(8,128)S(1)}, ...), condition=%wide.region_5.4_spmd.clone, body=%wide.region_3.3_spmd.clone.sunk | while | flops 534243 | bytes 1530784 | solution.py:71
  4879.9 1188.6 %collective-permute-start.6 = (f32[2,48,100,10]{2,1,0,3:T(8,128)}, f32[2,48,100,10]{2,1,0,3:T(8,128)}, u32[]{:S(2)}, u32[]{:S(2)}) collective-permute-start(f32[2,48,100,10]{2,1,0,3:T(8,128)} %get-tuple-element.3661), channel_id=1, source_target_pairs={{1,0},{2,1},{3,2},{5,4},{6,5},{7,6}} | collective-permute-start | bytes 1152008 | tf_op jit(solution)/shard_map/while/body/eval_jaxpr/ppermute | solution.py:130
  6114.8 7.5 copy.85
  6150.9 6709.8 %while.228 = (s32[]{:T(128)}, f32[2,48,100,10]{2,1,0,3:T(8,128)}, f32[2,24,100,10]{2,1,0,3:T(8,128)S(1)}, f32[2,24,48,10]{2,1,3,0:T(8,128)S(1)}, f32[270,2,24,48...) while((s32[]{:T(128)}, f32[2,48,100,10]{2,1,0,3:T(8,128)}, ...), condition=%wide.region_20.21_spmd, body=%wide.region_14.20_spmd.sunk | while | flops 1165991 | bytes 49494180 | solution.py:137
  6155.0 1182.8 %collective-permute-start.2 = (f32[2,48,100,10]{2,1,0,3:T(8,128)}, f32[2,48,100,10]{2,1,0,3:T(8,128)}, u32[]{:S(2)}, u32[]{:S(2)}) collective-permute-start(f32[2,48,100,10]{2,1,0,3:T(8,128)} %get-tuple-element.3706), channel_id=1, source_target_pairs={{1,0},{2,1},{3,2},{5,4},{6,5},{7,6}} | collective-permute-start | bytes 1152008 | tf_op jit(solution)/shard_map/while/body/eval_jaxpr/ppermute | solution.py:130
  7348.0 135.7 collective-permute-done.2
  7483.7 1330.5 %conditional.10 = (f32[170,2,24,48]{3,2,1,0:T(8,128)}, f32[2,48,100,10]{2,1,0,3:T(8,128)}, f32[2,24,100,10]{2,1,0,3:T(8,128)}, f32[2,24,48,10]{2,1,3,0:T(8,128)S(1)}, f32[1,2,48,100,10]{3,2,1,4,0:T(8,128)S(1)}) conditional(s32[]{:T(128)} %convert_element_type.96, f32[2,24,48,10]{2,1,3,0:T(8,128)S(1)} %get-tuple-element.4187, (s32[]{:T(128)}, ...), branch_computations={%region_15.15_spmd, %region_16.19_spmd} | conditional | flops 678297 | bytes 27037296 | solution.py:122
  7483.7 7.3 constant_dynamic-slice_fusion.4
  7500.8 1303.3 %while.224 = (s32[]{:T(128)}, f32[2,24,48,10]{2,1,3,0:T(8,128)S(1)}, f32[2,24,48,10]{2,1,3,0:T(8,128)S(1)}, f32[2,24,48,10]{2,1,3,0:T(8,128)S(1)}, f32[170,2,24,...) while((s32[]{:T(128)}, f32[2,24,48,10]{2,1,3,0:T(8,128)S(1)}, ...), condition=%wide.region_19.18_spmd.clone, body=%wide.region_17.17_spmd.clone.sunk | while | flops 534243 | bytes 1530784 | solution.py:71
  8824.5 1330.5 %conditional.10 = (f32[170,2,24,48]{3,2,1,0:T(8,128)}, f32[2,48,100,10]{2,1,0,3:T(8,128)}, f32[2,24,100,10]{2,1,0,3:T(8,128)}, f32[2,24,48,10]{2,1,3,0:T(8,128)S(1)}, f32[1,2,48,100,10]{3,2,1,4,0:T(8,128)S(1)}) conditional(s32[]{:T(128)} %convert_element_type.96, f32[2,24,48,10]{2,1,3,0:T(8,128)S(1)} %get-tuple-element.4187, (s32[]{:T(128)}, ...), branch_computations={%region_15.15_spmd, %region_16.19_spmd} | conditional | flops 678297 | bytes 27037296 | solution.py:122
  8824.5 7.3 constant_dynamic-slice_fusion.4
  8841.5 1303.3 %while.224 = (s32[]{:T(128)}, f32[2,24,48,10]{2,1,3,0:T(8,128)S(1)}, f32[2,24,48,10]{2,1,3,0:T(8,128)S(1)}, f32[2,24,48,10]{2,1,3,0:T(8,128)S(1)}, f32[170,2,24,...) while((s32[]{:T(128)}, f32[2,24,48,10]{2,1,3,0:T(8,128)S(1)}, ...), condition=%wide.region_19.18_spmd.clone, body=%wide.region_17.17_spmd.clone.sunk | while | flops 534243 | bytes 1530784 | solution.py:71
  10169.2 1328.3 %collective-permute-start.2 = (f32[2,48,100,10]{2,1,0,3:T(8,128)}, f32[2,48,100,10]{2,1,0,3:T(8,128)}, u32[]{:S(2)}, u32[]{:S(2)}) collective-permute-start(f32[2,48,100,10]{2,1,0,3:T(8,128)} %get-tuple-element.3706), channel_id=1, source_target_pairs={{1,0},{2,1},{3,2},{5,4},{6,5},{7,6}} | collective-permute-start | bytes 1152008 | tf_op jit(solution)/shard_map/while/body/eval_jaxpr/ppermute | solution.py:130
  11511.7 1327.6 %collective-permute-start.3 = (f32[2,24,100,10]{2,1,0,3:T(8,128)}, f32[2,24,100,10]{2,1,0,3:T(8,128)S(1)}, u32[]{:S(2)}, u32[]{:S(2)}) collective-permute-start(f32[2,24,100,10]{2,1,0,3:T(8,128)} %get-tuple-element.3707), channel_id=1, source_target_pairs={{0,4},{1,5},{2,6},{3,7}} | collective-permute-start | bytes 576008 | tf_op jit(solution)/shard_map/while/body/eval_jaxpr/ppermute | solution.py:131
  12883.3 7.5 copy.79
  12919.8 8512.7 %while.227 = (s32[]{:T(128)}, f32[2,48,100,10]{2,1,0,3:T(8,128)S(1)}, f32[2,24,100,10]{2,1,0,3:T(8,128)S(1)}, f32[2,24,48,10]{2,1,3,0:T(8,128)S(1)}, f32[270,2,2...) while((s32[]{:T(128)}, ...), condition=%wide.region_13.14_spmd, body=%wide.region_7.13_spmd.sunk | while | flops 1117991 | bytes 45684900 | solution.py:137
  12928.6 6.1 add_dynamic-update-slice_fusion.9
  12936.4 1315.8 %collective-permute-done.4 = f32[2,48,100,10]{2,1,0,3:T(8,128)S(1)} collective-permute-done((f32[2,48,100,10]{2,1,0,3:T(8,128)}, f32[2,48,100,10]{2,1,0,3:T(8,128)S(1)}, u32[]{:S(2)}, u32[]{:S(2)}) %collective-permute-start.4) | collective-permute-done | bytes 384032 | tf_op jit(solution)/shard_map/while/body/eval_jaxpr/ppermute | solution.py:130
  14259.2 6.1 add_dynamic-update-slice_fusion.9
  14273.2 6.1 add_dynamic-update-slice_fusion.9
  14279.4 3554.2 %collective-permute-done.5 = f32[2,24,100,10]{2,1,0,3:T(8,128)S(1)} collective-permute-done((f32[2,24,100,10]{2,1,0,3:T(8,128)}, f32[2,24,100,10]{2,1,0,3:T(8,128)S(1)}, u32[]{:S(2)}, u32[]{:S(2)}) %collective-permute-start.5) | collective-permute-done | bytes 192032 | tf_op jit(solution)/shard_map/while/body/eval_jaxpr/ppermute | solution.py:131
  17833.6 1191.3 %conditional.9 = (f32[170,2,24,48]{3,2,1,0:T(8,128)}, f32[2,48,100,10]{2,1,0,3:T(8,128)}, f32[2,24,100,10]{2,1,0,3:T(8,128)}, f32[2,24,48,10]{2,1,3,0:T(8,128)S(1)}, f32[1,2,24,100,10]{3,2,1,4,0:T(8,128)S(1)}) conditional(s32[]{:T(128)} %convert_element_type.95, f32[2,24,48,10]{2,1,3,0:T(8,128)S(1)} %get-tuple-element.4253, (s32[]{:T(128)}, ...), branch_computations={%region_8.8_spmd, %region_9.12_spmd} | conditional | flops 678297 | bytes 27037296 | solution.py:122
  17833.6 7.3 constant_dynamic-slice_fusion.2
  17849.2 1165.7 %while.223 = (s32[]{:T(128)}, f32[2,24,48,10]{2,1,3,0:T(8,128)S(1)}, f32[2,24,48,10]{2,1,3,0:T(8,128)S(1)}, f32[2,24,48,10]{2,1,3,0:T(8,128)S(1)}, f32[170,2,24,...) while((s32[]{:T(128)}, f32[2,24,48,10]{2,1,3,0:T(8,128)S(1)}, ...), condition=%wide.region_12.11_spmd.clone, body=%wide.region_10.10_spmd.clone.sunk | while | flops 534243 | bytes 1530784 | solution.py:71
  19028.2 6.1 add_dynamic-update-slice_fusion.9
  19035.1 1191.3 %conditional.9 = (f32[170,2,24,48]{3,2,1,0:T(8,128)}, f32[2,48,100,10]{2,1,0,3:T(8,128)}, f32[2,24,100,10]{2,1,0,3:T(8,128)}, f32[2,24,48,10]{2,1,3,0:T(8,128)S(1)}, f32[1,2,24,100,10]{3,2,1,4,0:T(8,128)S(1)}) conditional(s32[]{:T(128)} %convert_element_type.95, f32[2,24,48,10]{2,1,3,0:T(8,128)S(1)} %get-tuple-element.4253, (s32[]{:T(128)}, ...), branch_computations={%region_8.8_spmd, %region_9.12_spmd} | conditional | flops 678297 | bytes 27037296 | solution.py:122
  19035.1 7.3 constant_dynamic-slice_fusion.2
  19050.7 1165.7 %while.223 = (s32[]{:T(128)}, f32[2,24,48,10]{2,1,3,0:T(8,128)S(1)}, f32[2,24,48,10]{2,1,3,0:T(8,128)S(1)}, f32[2,24,48,10]{2,1,3,0:T(8,128)S(1)}, f32[170,2,24,...) while((s32[]{:T(128)}, f32[2,24,48,10]{2,1,3,0:T(8,128)S(1)}, ...), condition=%wide.region_12.11_spmd.clone, body=%wide.region_10.10_spmd.clone.sunk | while | flops 534243 | bytes 1530784 | solution.py:71
  20240.4 1183.1 %collective-permute-start.4 = (f32[2,48,100,10]{2,1,0,3:T(8,128)}, f32[2,48,100,10]{2,1,0,3:T(8,128)S(1)}, u32[]{:S(2)}, u32[]{:S(2)}) collective-permute-start(f32[2,48,100,10]{2,1,0,3:T(8,128)} %get-tuple-element.3684), channel_id=1, source_target_pairs={{0,1},{1,2},{2,3},{4,5},{5,6},{6,7}} | collective-permute-start | bytes 1152008 | tf_op jit(solution)/shard_map/while/body/eval_jaxpr/ppermute | solution.py:130
  21450.1 7.5 copy.91
  21483.6 5937.5 %while.229 = (s32[]{:T(128)}, f32[2,48,100,10]{2,1,0,3:T(8,128)S(1)}, f32[2,24,100,10]{2,1,0,3:T(8,128)S(1)}, f32[2,24,48,10]{2,1,3,0:T(8,128)S(1)}, f32[270,2,2...) while((s32[]{:T(128)}, ...), condition=%wide.region_27.28_spmd, body=%wide.region_21.27_spmd.sunk | while | flops 1069991 | bytes 41875564 | solution.py:137
  21513.1 1171.4 %collective-permute-done = f32[2,48,100,10]{2,1,0,3:T(8,128)S(1)} collective-permute-done((f32[2,48,100,10]{2,1,0,3:T(8,128)}, f32[2,48,100,10]{2,1,0,3:T(8,128)S(1)}, u32[]{:S(2)}, u32[]{:S(2)}) %collective-permute-start) | collective-permute-done | bytes 384032 | tf_op jit(solution)/shard_map/while/body/eval_jaxpr/ppermute | solution.py:130
  22684.4 1175.4 %conditional.11 = (f32[170,2,24,48]{3,2,1,0:T(8,128)}, f32[2,48,100,10]{2,1,0,3:T(8,128)}, f32[2,24,100,10]{2,1,0,3:T(8,128)}, f32[2,24,48,10]{2,1,3,0:T(8,128)S(1)}) conditional(s32[]{:T(128)} %convert_element_type.97, f32[2,24,48,10]{2,1,3,0:T(8,128)S(1)} %get-tuple-element.4319, (s32[]{:T(128)}, f32[270,2,24,48]{3,2,1,0:T(8,128)}, ...), branch_computations={%region_22.22_spmd, %region_23.26_spmd} | conditional | flops 678297 | bytes 27037292 | solution.py:122
  22684.5 7.4 constant_dynamic-slice_fusion.6
  22700.2 1149.7 %while.225 = (s32[]{:T(128)}, f32[2,24,48,10]{2,1,3,0:T(8,128)S(1)}, f32[2,24,48,10]{2,1,3,0:T(8,128)S(1)}, f32[2,24,48,10]{2,1,3,0:T(8,128)S(1)}, f32[170,2,24,...) while((s32[]{:T(128)}, f32[2,24,48,10]{2,1,3,0:T(8,128)S(1)}, ...), condition=%wide.region_26.25_spmd.clone, body=%wide.region_24.24_spmd.clone.sunk | while | flops 534243 | bytes 1530784 | solution.py:71
  23870.0 1175.4 %conditional.11 = (f32[170,2,24,48]{3,2,1,0:T(8,128)}, f32[2,48,100,10]{2,1,0,3:T(8,128)}, f32[2,24,100,10]{2,1,0,3:T(8,128)}, f32[2,24,48,10]{2,1,3,0:T(8,128)S(1)}) conditional(s32[]{:T(128)} %convert_element_type.97, f32[2,24,48,10]{2,1,3,0:T(8,128)S(1)} %get-tuple-element.4319, (s32[]{:T(128)}, f32[270,2,24,48]{3,2,1,0:T(8,128)}, ...), branch_computations={%region_22.22_spmd, %region_23.26_spmd} | conditional | flops 678297 | bytes 27037292 | solution.py:122
  23870.0 7.4 constant_dynamic-slice_fusion.6
  23885.7 1149.7 %while.225 = (s32[]{:T(128)}, f32[2,24,48,10]{2,1,3,0:T(8,128)S(1)}, f32[2,24,48,10]{2,1,3,0:T(8,128)S(1)}, f32[2,24,48,10]{2,1,3,0:T(8,128)S(1)}, f32[170,2,24,...) while((s32[]{:T(128)}, f32[2,24,48,10]{2,1,3,0:T(8,128)S(1)}, ...), condition=%wide.region_26.25_spmd.clone, body=%wide.region_24.24_spmd.clone.sunk | while | flops 534243 | bytes 1530784 | solution.py:71
  25059.6 1166.8 %collective-permute-start = (f32[2,48,100,10]{2,1,0,3:T(8,128)}, f32[2,48,100,10]{2,1,0,3:T(8,128)S(1)}, u32[]{:S(2)}, u32[]{:S(2)}) collective-permute-start(f32[2,48,100,10]{2,1,0,3:T(8,128)} %get-tuple-element.3728), channel_id=1, source_target_pairs={{0,1},{1,2},{2,3},{4,5},{5,6},{6,7}} | collective-permute-start | bytes 1152008 | tf_op jit(solution)/shard_map/while/body/eval_jaxpr/ppermute | solution.py:130
  26226.4 9.6 collective-permute-start.1
  26247.7 1167.5 %collective-permute-start.1 = (f32[2,24,100,10]{2,1,0,3:T(8,128)}, f32[2,24,100,10]{2,1,0,3:T(8,128)S(1)}, u32[]{:S(2)}, u32[]{:S(2)}) collective-permute-start(f32[2,24,100,10]{2,1,0,3:T(8,128)} %get-tuple-element.3729), channel_id=1, source_target_pairs={{0,4},{1,5},{2,6},{3,7}} | collective-permute-start | bytes 576008 | tf_op jit(solution)/shard_map/while/body/eval_jaxpr/ppermute | solution.py:131
  (22446 shorter events, 10326.6 us)
Async XLA Ops:
  73.7 11.3 collective-permute-start.6
  75.6 9.4 collective-permute-start.7
  88.9 2377.3 %collective-permute-start.6 = (f32[2,48,100,10]{2,1,0,3:T(8,128)}, f32[2,48,100,10]{2,1,0,3:T(8,128)}, u32[]{:S(2)}, u32[]{:S(2)}) collective-permute-start(f32[2,48,100,10]{2,1,0,3:T(8,128)} %get-tuple-element.3661), channel_id=1, source_target_pairs={{1,0},{2,1},{3,2},{5,4},{6,5},{7,6}} | collective-permute-start | bytes 1152008 | tf_op jit(solution)/shard_map/while/body/eval_jaxpr/ppermute | solution.py:130
  90.8 2375.4 %collective-permute-start.7 = (f32[2,24,100,10]{2,1,0,3:T(8,128)}, f32[2,24,100,10]{2,1,0,3:T(8,128)S(1)}, u32[]{:S(2)}, u32[]{:S(2)}) collective-permute-start(f32[2,24,100,10]{2,1,0,3:T(8,128)} %get-tuple-element.3662), channel_id=1, source_target_pairs={{4,0},{5,1},{6,2},{7,3}} | collective-permute-start | bytes 576008 | tf_op jit(solution)/shard_map/while/body/eval_jaxpr/ppermute | solution.py:131
  3659.1 11.4 collective-permute-start.6
  3661.1 9.4 collective-permute-start.7
  4863.5 12.6 collective-permute-start.6
  4865.4 10.7 collective-permute-start.7
  4879.9 1198.0 %collective-permute-start.6 = (f32[2,48,100,10]{2,1,0,3:T(8,128)}, f32[2,48,100,10]{2,1,0,3:T(8,128)}, u32[]{:S(2)}, u32[]{:S(2)}) collective-permute-start(f32[2,48,100,10]{2,1,0,3:T(8,128)} %get-tuple-element.3661), channel_id=1, source_target_pairs={{1,0},{2,1},{3,2},{5,4},{6,5},{7,6}} | collective-permute-start | bytes 1152008 | tf_op jit(solution)/shard_map/while/body/eval_jaxpr/ppermute | solution.py:130
  6068.5 9.4 collective-permute-start.7
  6081.8 12.1 collective-permute-start.6
  6083.7 10.1 collective-permute-start.7
  6155.0 1328.7 %collective-permute-start.2 = (f32[2,48,100,10]{2,1,0,3:T(8,128)}, f32[2,48,100,10]{2,1,0,3:T(8,128)}, u32[]{:S(2)}, u32[]{:S(2)}) collective-permute-start(f32[2,48,100,10]{2,1,0,3:T(8,128)} %get-tuple-element.3706), channel_id=1, source_target_pairs={{1,0},{2,1},{3,2},{5,4},{6,5},{7,6}} | collective-permute-start | bytes 1152008 | tf_op jit(solution)/shard_map/while/body/eval_jaxpr/ppermute | solution.py:130
  7337.8 10.3 collective-permute-start.3
  8814.2 9.4 collective-permute-start.2
  8816.1 7.4 collective-permute-start.3
  10155.0 9.4 collective-permute-start.2
  10156.9 7.5 collective-permute-start.3
  10169.2 1335.9 %collective-permute-start.2 = (f32[2,48,100,10]{2,1,0,3:T(8,128)}, f32[2,48,100,10]{2,1,0,3:T(8,128)}, u32[]{:S(2)}, u32[]{:S(2)}) collective-permute-start(f32[2,48,100,10]{2,1,0,3:T(8,128)} %get-tuple-element.3706), channel_id=1, source_target_pairs={{1,0},{2,1},{3,2},{5,4},{6,5},{7,6}} | collective-permute-start | bytes 1152008 | tf_op jit(solution)/shard_map/while/body/eval_jaxpr/ppermute | solution.py:130
  11497.5 7.5 collective-permute-start.3
  11509.8 1335.7 %collective-permute-start.2 = (f32[2,48,100,10]{2,1,0,3:T(8,128)}, f32[2,48,100,10]{2,1,0,3:T(8,128)}, u32[]{:S(2)}, u32[]{:S(2)}) collective-permute-start(f32[2,48,100,10]{2,1,0,3:T(8,128)} %get-tuple-element.3706), channel_id=1, source_target_pairs={{1,0},{2,1},{3,2},{5,4},{6,5},{7,6}} | collective-permute-start | bytes 1152008 | tf_op jit(solution)/shard_map/while/body/eval_jaxpr/ppermute | solution.py:130
  11511.7 1333.8 %collective-permute-start.3 = (f32[2,24,100,10]{2,1,0,3:T(8,128)}, f32[2,24,100,10]{2,1,0,3:T(8,128)S(1)}, u32[]{:S(2)}, u32[]{:S(2)}) collective-permute-start(f32[2,24,100,10]{2,1,0,3:T(8,128)} %get-tuple-element.3707), channel_id=1, source_target_pairs={{0,4},{1,5},{2,6},{3,7}} | collective-permute-start | bytes 576008 | tf_op jit(solution)/shard_map/while/body/eval_jaxpr/ppermute | solution.py:131
  12850.3 9.4 collective-permute-start.2
  12852.2 7.5 collective-permute-start.3
  12924.1 1328.1 %collective-permute-start.4 = (f32[2,48,100,10]{2,1,0,3:T(8,128)}, f32[2,48,100,10]{2,1,0,3:T(8,128)S(1)}, u32[]{:S(2)}, u32[]{:S(2)}) collective-permute-start(f32[2,48,100,10]{2,1,0,3:T(8,128)} %get-tuple-element.3684), channel_id=1, source_target_pairs={{0,1},{1,2},{2,3},{4,5},{5,6},{6,7}} | collective-permute-start | bytes 1152008 | tf_op jit(solution)/shard_map/while/body/eval_jaxpr/ppermute | solution.py:130
  12927.3 9.1 collective-permute-start.5
  14256.0 10.2 collective-permute-start.4
  14257.9 8.1 collective-permute-start.5
  14270.0 3563.6 %collective-permute-start.4 = (f32[2,48,100,10]{2,1,0,3:T(8,128)}, f32[2,48,100,10]{2,1,0,3:T(8,128)S(1)}, u32[]{:S(2)}, u32[]{:S(2)}) collective-permute-start(f32[2,48,100,10]{2,1,0,3:T(8,128)} %get-tuple-element.3684), channel_id=1, source_target_pairs={{0,1},{1,2},{2,3},{4,5},{5,6},{6,7}} | collective-permute-start | bytes 1152008 | tf_op jit(solution)/shard_map/while/body/eval_jaxpr/ppermute | solution.py:130
  14271.9 3561.7 %collective-permute-start.5 = (f32[2,24,100,10]{2,1,0,3:T(8,128)}, f32[2,24,100,10]{2,1,0,3:T(8,128)S(1)}, u32[]{:S(2)}, u32[]{:S(2)}) collective-permute-start(f32[2,24,100,10]{2,1,0,3:T(8,128)} %get-tuple-element.3685), channel_id=1, source_target_pairs={{4,0},{5,1},{6,2},{7,3}} | collective-permute-start | bytes 576008 | tf_op jit(solution)/shard_map/while/body/eval_jaxpr/ppermute | solution.py:131
  19024.9 10.2 collective-permute-start.4
  19026.8 8.3 collective-permute-start.5
  20226.4 10.1 collective-permute-start.4
  20228.4 8.1 collective-permute-start.5
  20240.4 1192.2 %collective-permute-start.4 = (f32[2,48,100,10]{2,1,0,3:T(8,128)}, f32[2,48,100,10]{2,1,0,3:T(8,128)S(1)}, u32[]{:S(2)}, u32[]{:S(2)}) collective-permute-start(f32[2,48,100,10]{2,1,0,3:T(8,128)} %get-tuple-element.3684), channel_id=1, source_target_pairs={{0,1},{1,2},{2,3},{4,5},{5,6},{6,7}} | collective-permute-start | bytes 1152008 | tf_op jit(solution)/shard_map/while/body/eval_jaxpr/ppermute | solution.py:130
  21423.4 9.1 collective-permute-start.5
  21487.6 11.6 collective-permute-start
  21489.5 9.7 collective-permute-start.1
  21502.9 1181.5 %collective-permute-start = (f32[2,48,100,10]{2,1,0,3:T(8,128)}, f32[2,48,100,10]{2,1,0,3:T(8,128)S(1)}, u32[]{:S(2)}, u32[]{:S(2)}) collective-permute-start(f32[2,48,100,10]{2,1,0,3:T(8,128)} %get-tuple-element.3728), channel_id=1, source_target_pairs={{0,1},{1,2},{2,3},{4,5},{5,6},{6,7}} | collective-permute-start | bytes 1152008 | tf_op jit(solution)/shard_map/while/body/eval_jaxpr/ppermute | solution.py:130
  21504.9 8.2 collective-permute-start.1
  23859.8 10.1 collective-permute-start
  23861.8 7.4 collective-permute-start.1
  25045.4 10.5 collective-permute-start
  25047.3 8.5 collective-permute-start.1
  25059.6 1182.5 %collective-permute-start = (f32[2,48,100,10]{2,1,0,3:T(8,128)}, f32[2,48,100,10]{2,1,0,3:T(8,128)S(1)}, u32[]{:S(2)}, u32[]{:S(2)}) collective-permute-start(f32[2,48,100,10]{2,1,0,3:T(8,128)} %get-tuple-element.3728), channel_id=1, source_target_pairs={{0,1},{1,2},{2,3},{4,5},{5,6},{6,7}} | collective-permute-start | bytes 1152008 | tf_op jit(solution)/shard_map/while/body/eval_jaxpr/ppermute | solution.py:130
  26226.4 15.6 collective-permute-start.1
  26245.8 1175.4 %collective-permute-start = (f32[2,48,100,10]{2,1,0,3:T(8,128)}, f32[2,48,100,10]{2,1,0,3:T(8,128)S(1)}, u32[]{:S(2)}, u32[]{:S(2)}) collective-permute-start(f32[2,48,100,10]{2,1,0,3:T(8,128)} %get-tuple-element.3728), channel_id=1, source_target_pairs={{0,1},{1,2},{2,3},{4,5},{5,6},{6,7}} | collective-permute-start | bytes 1152008 | tf_op jit(solution)/shard_map/while/body/eval_jaxpr/ppermute | solution.py:130
  26247.7 1173.5 %collective-permute-start.1 = (f32[2,24,100,10]{2,1,0,3:T(8,128)}, f32[2,24,100,10]{2,1,0,3:T(8,128)S(1)}, u32[]{:S(2)}, u32[]{:S(2)}) collective-permute-start(f32[2,24,100,10]{2,1,0,3:T(8,128)} %get-tuple-element.3729), channel_id=1, source_target_pairs={{0,4},{1,5},{2,6},{3,7}} | collective-permute-start | bytes 576008 | tf_op jit(solution)/shard_map/while/body/eval_jaxpr/ppermute | solution.py:131
  (48 other events, 7576.0 us)
where the time goes:
time: 27800 us; the launch traced here: 27500 us
  starting transfers between devices  8630 us (31%)
  waiting for transfers between devices  8550 us (31%)
  local copies, waits for them, and re-layouts  7730 us (28%)
  other arithmetic  2560 us (9%)
    ppermute x24, starting transfers between devices, stage_step(): lax.ppermute(out_x, 'x', perm_x)  6090 us
    ppermute x24, waiting for transfers between devices, stage_step(): lax.ppermute(out_y, 'y', perm_y)  5930 us
    dynamic_update_slice x2720, local copies, waits for them, and re-layouts, sweep_box(): lax.scan(plane_step, (zero_faces, zero_faces, z_in), (src_sk, sig_sk, xin...  3010 us
    ppermute x24, waiting for transfers between devices, stage_step(): lax.ppermute(out_x, 'x', perm_x)  2620 us
    ppermute x24, starting transfers between devices, stage_step(): lax.ppermute(out_y, 'y', perm_y)  2540 us
    broadcast_in_dim x1360, local copies, waits for them, and re-layouts, plane_step(): in_x = jnp.concatenate([edge_x[:, None], face_x[:, :-1]], axis=1)  1230 us
    add x1360, local copies, waits for them, and re-layouts, plane_step(): sig_t[..., None] + coef_sum  1030 us
    and x1360, other arithmetic, plane_step(): inside = ((z_level >= 0) & (z_level < size_l))[None, :, :, None]  869 us

commit v1 on v0

v1 whole, which is shorter than its diff:
```python
import functools

import jax
import jax.numpy as jnp
from jax import lax
from jax.experimental import pallas as pl
from jax.experimental.pallas import tpu as pltpu
from jax.sharding import PartitionSpec as P

F32 = jnp.float32
MESH = pl.DeviceIdType.MESH
NX, NY, NZ = 24, 48, 200
ND = 10
NB = NZ // 8
ROWS = NB * 72
D_NEAR = 8
D_FAR = 15
D_Y = 16
D_XR = 1
D_YR = 2
RING = 32
NSEND = 4


def x_lags():
    hops = [D_NEAR, D_FAR, D_NEAR, D_XR, D_NEAR, D_FAR, D_NEAR]
    lags = [0]
    for hop in hops:
        lags.append(lags[-1] + 8 + hop)
    return lags


def y_lags():
    lags = [0]
    for hop in [D_Y, D_YR, D_Y]:
        lags.append(lags[-1] + 16 + hop)
    return lags


LAG_X, LAG_Y = x_lags(), y_lags()
STEPS = ND * NB + LAG_X[-1] + LAG_Y[-1] + 7 + 15 + 1


def pick(values, idx):
    out = jnp.int32(values[0])
    for pos in range(1, len(values)):
        out = jnp.where(idx == pos, jnp.int32(values[pos]), out)
    return out


def kernel(cx_ref, cy_ref, cz_ref, wt_ref, src_ref, sig_ref, out_ref,
           nat, tab, flux, acc, hbuf, ctab, xbuf, ybuf, yraw, zbuf, eyb,
           xsend, xrecv, ysend, yrecv, v1ring, v2ring,
           xs_sem, xr_sem, ys_sem, yr_sem):
    dx = lax.axis_index("x")
    dy = lax.axis_index("y")
    has_left, has_right = dx > 0, dx < 3
    odd_x = lax.rem(dx, 2) == 1
    lag_left = jnp.where(odd_x, D_NEAR, D_FAR)
    lag_right = jnp.where(odd_x, D_FAR, D_NEAR)
    lane = lax.broadcasted_iota(jnp.int32, (8, 128), 1)
    subl = lax.broadcasted_iota(jnp.int32, (8, 128), 0)
    oct_id = lane // 16
    patch_y = lane - 16 * oct_id
    zero = jnp.zeros((8, 128), F32)
    low_half = lane < 64
    first_y = patch_y == 0

    lag_xm, lag_xp = pick(LAG_X[:4][::-1], dx), pick(LAG_X[4:], dx)
    lag_ym, lag_yp = pick(LAG_Y[:2][::-1], dy), pick(LAG_Y[2:], dy)
    lag_oct = (jnp.where(lane >= 64, lag_xp, lag_xm)
               + jnp.where((oct_id // 2) % 2 == 1, lag_yp, lag_ym))
    lag_lane = patch_y + lag_oct
    hbuf[...] = lag_lane + subl
    turn = lax.rem(lag_lane, NB)
    turn_bits = [(turn >> bit) & 1 == 1 for bit in range(5)]

    for pos in range(5):
        col = jnp.ones((8, 128), F32) if pos == 0 else zero
        for m in range(ND):
            two_x, two_y, two_z = 2.0 * cx_ref[m], 2.0 * cy_ref[m], 2.0 * cz_ref[m]
            val = (two_x + two_y + two_z, 2.0 * two_x, 2.0 * two_y, 2.0 * two_z, wt_ref[m])[pos]
            col = jnp.where(lane == m + 1, val, col)
        ctab[pos] = col

    for k in range(28):
        xbuf[pl.ds(8 * k, 8), :] = zero
    for k in range(24):
        ybuf[k] = zero
        eyb[k] = zero
    for k in range(12):
        yraw[k] = zero
    for k in range(9):
        zbuf[k] = zero
    for k in range(4):
        v1ring[k] = zero
        v2ring[k] = zero

    @pl.loop(0, RING)
    def _(k):
        for side in range(2):
            xrecv[side, k, pl.ds(0, 8), :] = zero
            xrecv[side, k, pl.ds(8, 8), :] = zero
        yrecv[k] = zero

    barrier = pltpu.get_barrier_semaphore()

    @pl.when(has_left)
    def _():
        pl.semaphore_signal(barrier, inc=1, device_id={"x": dx - 1}, device_id_type=MESH)

    @pl.when(has_right)
    def _():
        pl.semaphore_signal(barrier, inc=1, device_id={"x": dx + 1}, device_id_type=MESH)

    pl.semaphore_signal(barrier, inc=1, device_id={"y": 1 - dy}, device_id_type=MESH)

    mirror = (71 - lane) & 127
    tail = lane < 72

    @pl.loop(0, NX)
    def _(x):
        for arr, ref in enumerate((src_ref, sig_ref)):
            for yt in range(NY // 8):
                rows = pl.ds(8 * yt, 8)
                half_a = ref[x, rows, pl.ds(0, 128)]
                nat[arr, 0, x, rows, :] = half_a
                nat[arr, 1, x, rows, pl.ds(0, 72)] = ref[x, rows, pl.ds(128, 72)]
                half_b = nat[arr, 1, x, rows, :]
                flip_a = jnp.take_along_axis(half_a, mirror, axis=1)
                flip_b = jnp.take_along_axis(half_b, mirror, axis=1)
                nat[arr, 2, x, rows, :] = jnp.where(tail, flip_b, flip_a)
                nat[arr, 3, x, rows, :] = flip_a
        for part in range(8):
            for yt in range(NY // 8):
                acc[part, x, pl.ds(8 * yt, 8), :] = zero

    flip_rows = 7 - subl

    def row_groups(x_patch, i, j):
        for octant in range(8):
            bx, by = octant // 4, (octant // 2) % 2
            x_rel = 3 * x_patch + i
            x_abs = x_rel if bx else NX - 1 - x_rel
            for half in range(2):
                y_abs = (24 * half + j) if by else (26 - 24 * half - j)
                yield octant, half, x_abs, y_abs, by == 0

    def turn_blocks(blocks, step):
        for bit in range(5):
            shift = step * (1 << bit)
            blocks = [jnp.where(turn_bits[bit], blocks[(v - shift) % NB], blocks[v]) for v in range(NB)]
        return blocks

    @pl.loop(0, 8)
    def _(xp):
        for i in range(3):
            for j in range(3):
                cell = 3 * i + j
                for arr in range(2):
                    pieces = [[], []]
                    for octant, half, x_abs, y_abs, rev in row_groups(xp, i, j):
                        for zh in range(2):
                            kind = zh + (0 if octant % 2 else 2)
                            val = nat[arr, kind, x_abs, pl.ds(y_abs, 8, stride=3), :]
                            if rev:
                                val = jnp.take_along_axis(val, flip_rows, axis=0)
                            pieces[zh].append(val)
                    lo = jnp.concatenate(pieces[0], axis=0).T
                    hi = jnp.concatenate(pieces[1], axis=0).T
                    blocks = [lo[8 * v:8 * v + 8] for v in range(16)] + [hi[8 * v:8 * v + 8] for v in range(9)]
                    blocks = turn_blocks(blocks, 1)
                    for v in range(NB):
                        start = lax.rem(v + xp, NB) * 72 + xp
                        tab[arr, cell, pl.ds(start, 8, stride=9), :] = blocks[v]
                        if arr == 0:
                            flux[cell, pl.ds(start, 8, stride=9), :] = zero

    pl.semaphore_wait(barrier, has_left.astype(jnp.int32) + has_right.astype(jnp.int32) + 1)

    from_neg = ((oct_id + 1) // 2) % 2
    keep_send = from_neg == dy
    keep_recv = from_neg == 1 - dy
    mirror_y = dy == 0
    mirror_x = dx == 0

    def x_copy(side, n):
        lag = lag_left if side == 0 else lag_right
        slot = lax.rem(n + lag, RING)
        return pltpu.make_async_remote_copy(
            src_ref=xsend.at[side, lax.rem(n, NSEND)], dst_ref=xrecv.at[side, slot],
            send_sem=xs_sem.at[side, lax.rem(n, NSEND)], recv_sem=xr_sem.at[side, slot],
            device_id={"x": dx - 1 if side == 0 else dx + 1}, device_id_type=MESH)

    def y_copy(n):
        slot = lax.rem(n - 1 + D_Y, RING)
        return pltpu.make_async_remote_copy(
            src_ref=ysend.at[lax.rem(n, NSEND)], dst_ref=yrecv.at[slot],
            send_sem=ys_sem.at[lax.rem(n, NSEND)], recv_sem=yr_sem.at[slot],
            device_id={"y": 1 - dy}, device_id_type=MESH)

    def x_sends(side, n):
        has, lag = (has_left, lag_left) if side == 0 else (has_right, lag_right)
        return has & (n >= 1) & (n + lag <= STEPS - 1)

    def y_sends(n):
        return (n >= 2) & (n - 1 + D_Y <= STEPS - 1)

    def x_waits(side, n):
        has, lag = (has_right, lag_right) if side == 0 else (has_left, lag_left)
        return has & (n >= lag) & (n + 1 <= STEPS - 1)

    def y_waits(n):
        return (n >= D_Y) & (n + 1 <= STEPS - 1)

    def step(n, carry):
        next_slot = lax.rem(n + 1, RING)
        send_slot = lax.rem(n, NSEND)

        for side in range(2):
            @pl.when(x_waits(side, n))
            def _(side=side):
                pltpu.make_async_remote_copy(
                    src_ref=xsend.at[side, 0], dst_ref=xrecv.at[side, next_slot],
                    send_sem=xs_sem.at[side, 0], recv_sem=xr_sem.at[side, next_slot],
                    device_id={"x": dx}, device_id_type=MESH).wait_recv()

            @pl.when(x_sends(side, n - NSEND))
            def _(side=side):
                x_copy(side, n - NSEND).wait_send()

        @pl.when(y_waits(n))
        def _():
            pltpu.make_async_remote_copy(
                src_ref=ysend.at[0], dst_ref=yrecv.at[next_slot],
                send_sem=ys_sem.at[0], recv_sem=yr_sem.at[next_slot],
                device_id={"y": dy}, device_id_type=MESH).wait_recv()

        @pl.when(y_sends(n - NSEND))
        def _():
            y_copy(n - NSEND).wait_send()

        msg_slot = lax.rem(n + 2, 4)
        v1_old, v2_old = v1ring[msg_slot], v2ring[msg_slot]
        ysend[send_slot] = jnp.where(keep_send, v1_old, v2_old)

        outs = [xbuf[pl.ds(72 * q + 8, 8, stride=9), :] for q in range(3)]
        swapped = pltpu.roll(outs[1], 64, 1)
        left_a = jnp.where(low_half, outs[0], swapped)
        right_a = jnp.where(low_half, swapped, outs[0])
        xsend[0, send_slot, pl.ds(0, 8), :] = left_a
        xsend[0, send_slot, pl.ds(8, 8), :] = outs[2]
        xsend[1, send_slot, pl.ds(0, 8), :] = right_a
        xsend[1, send_slot, pl.ds(8, 8), :] = outs[2]

        from_r_a, from_r_b = xrecv[0, next_slot, pl.ds(0, 8), :], xrecv[0, next_slot, pl.ds(8, 8), :]
        from_l_a = jnp.where(mirror_x, pltpu.roll(left_a, 64, 1), xrecv[1, next_slot, pl.ds(0, 8), :])
        from_l_b = jnp.where(mirror_x, pltpu.roll(outs[2], 64, 1), xrecv[1, next_slot, pl.ds(8, 8), :])
        edges = [jnp.where(low_half, from_r_a, from_l_a),
                 pltpu.roll(jnp.where(low_half, from_l_a, from_r_a), 64, 1),
                 jnp.where(low_half, from_r_b, from_l_b)]

        pack2 = lax.rem(n + 3, 4)
        for k in range(12):
            raw = yraw[k]
            ybuf[12 + k] = jnp.where(first_y, eyb[12 + k], pltpu.roll(raw, 1, 1))
            pltpu.store(v2ring.at[pack2], pltpu.roll(raw, (33 + k) % 128, 1), mask=patch_y == k)

        got = yrecv[next_slot]
        in1 = jnp.where(keep_recv, got, jnp.where(mirror_y, pltpu.roll(v1_old, 32, 1), 0.0))
        in2 = jnp.where(keep_recv, pltpu.roll(got, 96, 1), jnp.where(mirror_y, v2_old, 0.0))
        new_ey = [pltpu.roll(in1, 112 - k, 1) for k in range(12)]
        for k in range(12):
            eyb[12 + k] = pltpu.roll(in2, 112 - k, 1)

        late = n - hbuf[...]
        m_idx = (late * 1311) >> 15
        fresh = late == m_idx * NB
        c_idx = jnp.clip(m_idx + 1, 0, ND + 1)
        asum, ax, ay, az, wt = [jnp.take_along_axis(ctab[pos], c_idx, axis=1) for pos in range(5)]

        base = lax.rem(n, NB) * 72
        z_face = [jnp.where(fresh, 0.0, zbuf[c]) for c in range(9)]
        pack1 = lax.rem(n, 4)
        for s in range(8):
            rows = pl.ds(base + 9 * s, 8)
            x_face = [xbuf[pl.ds(9 * (3 * s + j), 8), :] for j in range(3)]
            for i in range(3):
                k = 3 * s + i
                y_face = ybuf[k]
                for j in range(3):
                    c = 3 * i + j
                    total = ((tab[0, c, rows, :] + z_face[c]) + x_face[j]) + y_face
                    psi = total * (1.0 / (tab[1, c, rows, :] + asum))
                    x_face[j] = ax * psi - x_face[j]
                    y_face = ay * psi - y_face
                    z_face[c] = az * psi - z_face[c]
                    flux[c, rows, :] = flux[c, rows, :] + wt * psi
                if s < 4:
                    shifted = pltpu.roll(y_face, 1, 1)
                    ybuf[k] = jnp.where(first_y, new_ey[k], shifted)
                    packed = shifted if k == 0 else pltpu.roll(y_face, 1 + k, 1)
                    pltpu.store(v1ring.at[pack1], packed, mask=patch_y == k)
                else:
                    yraw[k - 12] = y_face
            for j in range(3):
                xbuf[pl.ds(9 * (3 * s + j) + 1, 8), :] = x_face[j]
            if s == 3:
                for side in range(2):
                    @pl.when(x_sends(side, n))
                    def _(side=side):
                        x_copy(side, n).start()

                @pl.when(y_sends(n))
                def _():
                    y_copy(n).start()
        for c in range(9):
            zbuf[c] = z_face[c]
        for q in range(3):
            xbuf[pl.ds(72 * q, 8, stride=9), :] = edges[q]
        return carry

    lax.fori_loop(0, STEPS, step, 0)

    for back in range(NSEND, 0, -1):
        n = STEPS - back
        for side in range(2):
            @pl.when(x_sends(side, jnp.int32(n)))
            def _(side=side, n=n):
                x_copy(side, jnp.int32(n)).wait_send()

        @pl.when(y_sends(jnp.int32(n)))
        def _(n=n):
            y_copy(jnp.int32(n)).wait_send()

    @pl.loop(0, 8)
    def _(xp):
        for i in range(3):
            for j in range(3):
                cell = 3 * i + j
                blocks = [flux[cell, pl.ds(lax.rem(v + xp, NB) * 72 + xp, 8, stride=9), :] for v in range(NB)]
                blocks = turn_blocks(blocks, -1)
                lo = jnp.concatenate(blocks[:16], axis=0).T
                hi = jnp.concatenate(blocks[16:] + [zero] * 7, axis=0).T
                parts, olds = [], []
                for octant, half, x_abs, y_abs, rev in row_groups(xp, i, j):
                    for zh in range(2):
                        part = 4 * (octant % 2) + 2 * ((octant // 2) % 2) + zh
                        row = 16 * octant + 8 * half
                        val = (lo, hi)[zh][row:row + 8]
                        if rev:
                            val = jnp.take_along_axis(val, flip_rows, axis=0)
                        where = (part, x_abs, pl.ds(y_abs, 8, stride=3))
                        olds.append(acc[where + (slice(None),)] + val)
                        parts.append(where)
                for where, val in zip(parts, olds):
                    acc[where + (slice(None),)] = val

    @pl.loop(0, NX)
    def _(x):
        for yt in range(NY // 8):
            rows = pl.ds(8 * yt, 8)
            up_a = acc[4, x, rows, :] + acc[6, x, rows, :]
            up_b = acc[5, x, rows, :] + acc[7, x, rows, :]
            dn_a = jnp.take_along_axis(acc[0, x, rows, :] + acc[2, x, rows, :], mirror, axis=1)
            dn_b = jnp.take_along_axis(acc[1, x, rows, :] + acc[3, x, rows, :], mirror, axis=1)
            out_ref[x, rows, pl.ds(0, 128)] = up_a + jnp.where(tail, dn_b, dn_a)
            out_ref[x, rows, pl.ds(128, 72)] = (up_b + dn_a)[:, :72]


def solution(mesh):
    grid_spec = P(("g", "x"), "y", None)

    def column_sweep(source, sigma_t, cos_x, cos_y, cos_z, weights):
        smem = pl.BlockSpec(memory_space=pltpu.SMEM)
        vmem = pl.BlockSpec(memory_space=pltpu.VMEM)
        return pl.pallas_call(
            kernel,
            out_shape=jax.ShapeDtypeStruct((NX, NY, NZ), F32),
            in_specs=[smem] * 4 + [vmem] * 2,
            out_specs=vmem,
            scratch_shapes=[
                pltpu.VMEM((2, 4, NX, NY, 128), F32),
                pltpu.VMEM((2, 9, ROWS, 128), F32),
                pltpu.VMEM((9, ROWS, 128), F32),
                pltpu.VMEM((8, NX, NY, 128), F32),
                pltpu.VMEM((8, 128), jnp.int32),
                pltpu.VMEM((5, 8, 128), F32),
                pltpu.VMEM((224, 128), F32),
                pltpu.VMEM((24, 8, 128), F32),
                pltpu.VMEM((12, 8, 128), F32),
                pltpu.VMEM((9, 8, 128), F32),
                pltpu.VMEM((24, 8, 128), F32),
                pltpu.VMEM((2, NSEND, 16, 128), F32),
                pltpu.VMEM((2, RING, 16, 128), F32),
                pltpu.VMEM((NSEND, 8, 128), F32),
                pltpu.VMEM((RING, 8, 128), F32),
                pltpu.VMEM((4, 8, 128), F32),
                pltpu.VMEM((4, 8, 128), F32),
                pltpu.SemaphoreType.DMA((2, NSEND)),
                pltpu.SemaphoreType.DMA((2, RING)),
                pltpu.SemaphoreType.DMA((NSEND,)),
                pltpu.SemaphoreType.DMA((RING,)),
            ],
            compiler_params=pltpu.CompilerParams(
                collective_id=0, has_side_effects=True, vmem_limit_bytes=60 * 1024 * 1024),
        )(cos_x, cos_y, cos_z, weights, source, sigma_t)

    return jax.shard_map(column_sweep, mesh=mesh, in_specs=(grid_spec, grid_spec, P(), P(), P(), P()),
                         out_specs=grid_spec, check_vma=False)
```

time: 27800 us -> 211 us (0.01)
  starting transfers between devices: 8630 us -> 0 us
  waiting for transfers between devices: 8550 us -> 0 us
  local copies, waits for them, and re-layouts: 7730 us -> 2.36 us
  other arithmetic: 2560 us -> 0 us
    ppermute x48 -> x0, starting transfers between devices: 8630 us -> none  [the longest x24 6090 us: stage_step(): lax.ppermute(out_x, 'x', perm_x)]
    ppermute x48 -> x0, waiting for transfers between devices: 8550 us -> none  [the longest x24 5930 us: stage_step(): lax.ppermute(out_y, 'y', perm_y)]
    dynamic_update_slice x2720 -> x0, local copies, waits for them, and re-layouts: 3010 us -> none  [sweep_box(): lax.scan(plane_step, (zero_faces, zero_faces, z_in), (src_sk, sig_sk, xin...]
    broadcast_in_dim x5468 -> x0, local copies, waits for them, and re-layouts: 1770 us -> none  [the longest x1360 1230 us: plane_step(): in_x = jnp.concatenate([edge_x[:, None], face_x[:, :-1]], axis=1)]
    add x1360 -> x0, local copies, waits for them, and re-layouts: 1030 us -> none  [plane_step(): sig_t[..., None] + coef_sum]
    dynamic_update_slice x1384 -> x0, other arithmetic: 979 us -> none  [the longest x1360 834 us: sweep_box(): lax.scan(plane_step, (zero_faces, zero_faces, z_in), (src_sk, sig_sk, xin...]
    dynamic_slice x1368 -> x0, local copies, waits for them, and re-layouts: 900 us -> none  [the longest x1360 842 us: sweep_box(): lax.scan(plane_step, (zero_faces, zero_faces, z_in), (src_sk, sig_sk, xin...]
    and x1360 -> x0, other arithmetic: 869 us -> none  [plane_step(): inside = ((z_level >= 0) & (z_level < size_l))[None, :, :, None]]
where the time goes in v1:
time: 211 us
  Pallas kernels  209 us (99%)
  local copies, waits for them, and re-layouts  2.36 us (1%)
    pallas_call x1, Pallas kernels, column_sweep(): pl.pallas_call(kernel, out_shape=jax.ShapeDtypeStruct((NX, NY, NZ), F32),...  209 us

profile of v1, /device:TPU:2, one launch (start us, length us, event | category | flops | bytes accessed | tf_op | source)
XLA Modules:
  0.0 211.0 jit_solution(4875325665185265267)
XLA Ops:
  0.0 208.7 %shard_map.64 = f32[24,48,200]{2,1,0:T(8,128)} custom-call(f32[10]{0:T(128)} %cx_ref.1, f32[10]{0:T(128)} %cy_ref.1, f32[10]{0:T(128)} %cz_ref.1, f32[10]{0:T(128)} %wt_ref.1, f32[24,48,200]{2,1,0:T(8,128)} %src_ref.1, f32[24,48,200]{2,1,0:T(8,128)} %sig_ref.1), custom_call_target="tpu_custom_call" | custom-call | tf_op jit(solution)/shard_map/pallas_call | solution.py:377
  208.7 2.4 %copy.8 = f32[24,48,200]{2,1,0:T(8,128)} copy(f32[24,48,200]{2,1,0:T(8,128)} %shard_map.64) | data formatting | bytes 1843200

commit v2 on v1

v2 whole, which is shorter than its diff:
```python
import functools

import jax
import jax.numpy as jnp
from jax import lax
from jax.experimental import pallas as pl
from jax.experimental.pallas import tpu as pltpu
from jax.sharding import PartitionSpec as P

F32 = jnp.float32
MESH = pl.DeviceIdType.MESH
NX, NY, NZ = 24, 48, 200
ND = 10
NB = NZ // 8
ROWS = NB * 72
T_NEAR = 7
T_FAR = 14
T_Y = 14
D_XR = 1
D_YR = 2
RING = 32
NSEND = 8
SPOTS = [2, 13, 3, 4, 11, 12, 5, 10, 6, 7, 8, 9]
PARTNER = [SPOTS.index(15 - spot) for spot in SPOTS]


def x_lags():
    near, far = T_NEAR + 1, T_FAR + 1
    hops = [near, far, near, D_XR, near, far, near]
    lags = [0]
    for hop in hops:
        lags.append(lags[-1] + 8 + hop)
    return lags


def y_lags():
    lags = [0]
    for hop in [T_Y + 2, D_YR, T_Y + 2]:
        lags.append(lags[-1] + 16 + hop)
    return lags


LAG_X, LAG_Y = x_lags(), y_lags()
STEPS = ND * NB + LAG_X[-1] + LAG_Y[-1] + 7 + 15 + 1


def pick(values, idx):
    out = jnp.int32(values[0])
    for pos in range(1, len(values)):
        out = jnp.where(idx == pos, jnp.int32(values[pos]), out)
    return out


def kernel(cx_ref, cy_ref, cz_ref, wt_ref, src_ref, sig_ref, out_ref,
           nat, tab, flux, acc, hbuf, ctab, ntab, cbuf, xbuf, ybuf, yraw, zbuf, inodd, refl,
           xsend, xrecv, ysend, yrecv, pack,
           xs_sem, xr_sem, ys_sem, yr_sem):
    dx = lax.axis_index("x")
    dy = lax.axis_index("y")
    has_left, has_right = dx > 0, dx < 3
    odd_x = (dx & 1) == 1
    trip_left = jnp.where(odd_x, T_NEAR, T_FAR)
    trip_right = jnp.where(odd_x, T_FAR, T_NEAR)
    lane = lax.broadcasted_iota(jnp.int32, (8, 128), 1)
    subl = lax.broadcasted_iota(jnp.int32, (8, 128), 0)
    oct_id = lane // 16
    oct_y = (oct_id // 2) % 2
    patch_y = lane - 16 * oct_id
    zero = jnp.zeros((8, 128), F32)
    low_half = lane < 64
    first_y = patch_y == 0

    lag_xm, lag_xp = pick(LAG_X[:4][::-1], dx), pick(LAG_X[4:], dx)
    lag_ym, lag_yp = pick(LAG_Y[:2][::-1], dy), pick(LAG_Y[2:], dy)
    lag_oct = jnp.where(lane >= 64, lag_xp, lag_xm) + jnp.where(oct_y == 1, lag_yp, lag_ym)
    lag_lane = patch_y + lag_oct
    hbuf[...] = lax.rem(lag_lane + subl, NB)
    turn = lax.rem(lag_lane, NB)
    turn_bits = [(turn >> bit) & 1 == 1 for bit in range(5)]

    for pos in range(5):
        col = jnp.ones((8, 128), F32) if pos == 0 else zero
        for m in range(ND):
            two_x, two_y, two_z = 2.0 * cx_ref[m], 2.0 * cy_ref[m], 2.0 * cz_ref[m]
            val = (two_x + two_y + two_z, 2.0 * two_x, 2.0 * two_y, 2.0 * two_z, wt_ref[m])[pos]
            col = jnp.where(lane == m + 1, val, col)
        ctab[pos] = col
        cbuf[pos] = jnp.ones((8, 128), F32) if pos == 0 else zero

    @pl.loop(0, ntab.shape[1] // 8)
    def _(k):
        late = 8 * k + subl - lag_oct
        c_idx = jnp.clip(((late * 1311) >> 15) + 1, 0, ND + 1)
        for pos in range(5):
            ntab[pos, pl.ds(8 * k, 8), :] = jnp.take_along_axis(ctab[pos], c_idx, axis=1)

    for k in range(28):
        xbuf[pl.ds(8 * k, 8), :] = zero
    for k in range(24):
        ybuf[k] = zero
    for k in range(12):
        yraw[k] = zero
    for k in range(9):
        zbuf[k] = zero
    inodd[...] = zero
    refl[...] = zero
    for k in range(4):
        pack[k, 0] = zero
        pack[k, 1] = zero

    @pl.loop(0, RING)
    def _(k):
        for side in range(2):
            for q in range(3):
                xrecv[side, k, pl.ds(8 * q, 8), :] = zero
        yrecv[k] = zero

    barrier = pltpu.get_barrier_semaphore()

    @pl.when(has_left)
    def _():
        pl.semaphore_signal(barrier, inc=1, device_id={"x": dx - 1}, device_id_type=MESH)

    @pl.when(has_right)
    def _():
        pl.semaphore_signal(barrier, inc=1, device_id={"x": dx + 1}, device_id_type=MESH)

    pl.semaphore_signal(barrier, inc=1, device_id={"y": 1 - dy}, device_id_type=MESH)

    mirror = (71 - lane) & 127
    tail = lane < 72

    @pl.loop(0, NX)
    def _(x):
        for arr, ref in enumerate((src_ref, sig_ref)):
            for yt in range(NY // 8):
                rows = pl.ds(8 * yt, 8)
                half_a = ref[x, rows, pl.ds(0, 128)]
                nat[arr, 0, x, rows, :] = half_a
                nat[arr, 1, x, rows, pl.ds(0, 72)] = ref[x, rows, pl.ds(128, 72)]
                half_b = nat[arr, 1, x, rows, :]
                flip_a = jnp.take_along_axis(half_a, mirror, axis=1)
                flip_b = jnp.take_along_axis(half_b, mirror, axis=1)
                nat[arr, 2, x, rows, :] = jnp.where(tail, flip_b, flip_a)
                nat[arr, 3, x, rows, :] = flip_a
        for part in range(8):
            for yt in range(NY // 8):
                acc[part, x, pl.ds(8 * yt, 8), :] = zero

    flip_rows = 7 - subl

    def row_groups(x_patch, i, j):
        for octant in range(8):
            bx, by = octant // 4, (octant // 2) % 2
            x_rel = 3 * x_patch + i
            x_abs = x_rel if bx else NX - 1 - x_rel
            for half in range(2):
                y_abs = (24 * half + j) if by else (26 - 24 * half - j)
                yield octant, half, x_abs, y_abs, by == 0

    def turn_blocks(blocks, step):
        for bit in range(5):
            shift = step * (1 << bit)
            blocks = [jnp.where(turn_bits[bit], blocks[(v - shift) % NB], blocks[v]) for v in range(NB)]
        return blocks

    @pl.loop(0, 8)
    def _(xp):
        for i in range(3):
            for j in range(3):
                cell = 3 * i + j
                for arr in range(2):
                    pieces = [[], []]
                    for octant, half, x_abs, y_abs, rev in row_groups(xp, i, j):
                        for zh in range(2):
                            kind = zh + (0 if octant % 2 else 2)
                            val = nat[arr, kind, x_abs, pl.ds(y_abs, 8, stride=3), :]
                            if rev:
                                val = jnp.take_along_axis(val, flip_rows, axis=0)
                            pieces[zh].append(val)
                    lo = jnp.concatenate(pieces[0], axis=0).T
                    hi = jnp.concatenate(pieces[1], axis=0).T
                    blocks = [lo[8 * v:8 * v + 8] for v in range(16)] + [hi[8 * v:8 * v + 8] for v in range(9)]
                    blocks = turn_blocks(blocks, 1)
                    for v in range(NB):
                        start = lax.rem(v + xp, NB) * 72 + xp
                        tab[arr, cell, pl.ds(start, 8, stride=9), :] = blocks[v]
                        if arr == 0:
                            flux[cell, pl.ds(start, 8, stride=9), :] = zero

    pl.semaphore_wait(barrier, has_left.astype(jnp.int32) + has_right.astype(jnp.int32) + 1)

    keep_send = oct_y == 1 - dy
    even_mask, odd_mask = oct_y == dy, oct_y == 1 - dy
    mirror_x, mirror_y = dx == 0, dy == 0
    has = (has_left, has_right, True)
    trips = (trip_left, trip_right, T_Y)

    def copy(kind, n):
        slot, here = (n + trips[kind]) & (RING - 1), n & (NSEND - 1)
        if kind == 2:
            return pltpu.make_async_remote_copy(
                src_ref=ysend.at[here], dst_ref=yrecv.at[slot], send_sem=ys_sem.at[here], recv_sem=yr_sem.at[slot],
                device_id={"y": 1 - dy}, device_id_type=MESH)
        return pltpu.make_async_remote_copy(
            src_ref=xsend.at[here], dst_ref=xrecv.at[kind, slot],
            send_sem=xs_sem.at[kind, here], recv_sem=xr_sem.at[kind, slot],
            device_id={"x": dx - 1 if kind == 0 else dx + 1}, device_id_type=MESH)

    def arrival(kind, n):
        slot = n & (RING - 1)
        if kind == 2:
            return pltpu.make_async_remote_copy(
                src_ref=ysend.at[0], dst_ref=yrecv.at[slot], send_sem=ys_sem.at[0], recv_sem=yr_sem.at[slot],
                device_id={"y": dy}, device_id_type=MESH)
        return pltpu.make_async_remote_copy(
            src_ref=xsend.at[0], dst_ref=xrecv.at[kind, slot], send_sem=xs_sem.at[kind, 0],
            recv_sem=xr_sem.at[kind, slot], device_id={"x": dx}, device_id_type=MESH)

    def when(cond, act):
        if cond is True:
            act()
        else:
            pl.when(cond)(act)

    def both(one, two):
        return two if one is True else (one if two is True else one & two)

    def sends(kind, n, full):
        if not full:
            return has[kind]
        return both(has[kind], (n >= 2) & (n + trips[kind] <= STEPS - 2))

    def waits(kind, n, full):
        if not full:
            return (has_right, has_left, True)[kind]
        trip = (trip_right, trip_left, T_Y)[kind]
        return both((has_right, has_left, True)[kind], (n >= trip + 2) & (n <= STEPS - 2))

    def step(n, base, full):
        here = n & (NSEND - 1)
        slot = n & (RING - 1)
        now, last, before = n & 3, (n + 3) & 3, (n + 2) & 3

        outs = [xbuf[pl.ds(72 * q + 8, 8, stride=9), :] for q in range(3)]
        pack_even, pack_odd = pack[before, 0], pack[before, 1]
        for kind in range(3):
            when(sends(kind, n - NSEND, full), lambda kind=kind: copy(kind, n - NSEND).wait_send())
        for q in range(3):
            xsend[here, pl.ds(8 * q, 8), :] = outs[q]
        ysend[here] = jnp.where(keep_send, pack_even, pack_odd)
        for kind in range(3):
            when(sends(kind, n, full), lambda kind=kind: copy(kind, n).start())
        for kind in range(3):
            when(waits(kind, n, full), lambda kind=kind: arrival(kind, n).wait_recv())

        edges = []
        for q in range(3):
            rows = pl.ds(8 * q, 8)
            from_left = jnp.where(mirror_x, pltpu.roll(outs[q], 64, 1), xrecv[1, slot, rows, :])
            edges.append(jnp.where(low_half, xrecv[0, slot, rows, :], from_left))
        got = yrecv[slot]
        in_even = jnp.where(even_mask, got, refl[...])
        in_odd = inodd[...]
        refl[...] = jnp.where(mirror_y, pltpu.roll(pack[last, 0], 32, 1), 0.0)
        inodd[...] = jnp.where(odd_mask, pltpu.roll(got, 64, 1),
                               jnp.where(mirror_y, pltpu.roll(pack_odd, 96, 1), 0.0))

        mains, mixes = {}, {}

        def serve(level, faces, odd):
            for i in range(3):
                f = 3 * (level % 4) + i
                spot = SPOTS[f]
                mains[f] = pltpu.roll(faces[i], 1, 1)
                mixed = jnp.where(patch_y == 15 - spot, in_odd if odd else in_even, faces[i])
                mixes[PARTNER[f]] = pltpu.roll(mixed, (1 + spot + (16 if odd else 112)) % 128, 1)
                pltpu.store(pack.at[last if odd else now, 1 if odd else 0], mixes[PARTNER[f]], mask=patch_y == spot)
            for f in [f for f in mains if f in mixes]:
                ybuf[f + (12 if odd else 0)] = jnp.where(first_y, mixes.pop(f), mains.pop(f))

        for level in range(4):
            serve(level, [yraw[3 * level + i] for i in range(3)], True)

        fresh = hbuf[...] == lax.div(base, 72)
        coef = []
        for pos in range(5):
            coef.append(jnp.where(fresh, ntab[pos, pl.ds(n, 1), :], cbuf[pos]))
            cbuf[pos] = coef[pos]
        asum, ax, ay, az, wt = coef
        z_face = [jnp.where(fresh, 0.0, zbuf[c]) for c in range(9)]

        for s in range(8):
            rows = pl.ds(base + 9 * s, 8)
            x_face = [xbuf[pl.ds(9 * (3 * s + j), 8), :] for j in range(3)]
            y_out = []
            for i in range(3):
                y_face = ybuf[3 * s + i]
                for j in range(3):
                    c = 3 * i + j
                    total = ((tab[0, c, rows, :] + z_face[c]) + x_face[j]) + y_face
                    psi = total * (1.0 / (tab[1, c, rows, :] + asum))
                    x_face[j] = ax * psi - x_face[j]
                    y_face = ay * psi - y_face
                    z_face[c] = az * psi - z_face[c]
                    flux[c, rows, :] = flux[c, rows, :] + wt * psi
                y_out.append(y_face)
            if s < 4:
                serve(s, y_out, False)
            else:
                for i in range(3):
                    yraw[3 * (s - 4) + i] = y_out[i]
            for j in range(3):
                xbuf[pl.ds(9 * (3 * s + j) + 1, 8), :] = x_face[j]
        for c in range(9):
            zbuf[c] = z_face[c]
        for q in range(3):
            xbuf[pl.ds(72 * q, 8, stride=9), :] = edges[q]
        return jnp.where(base == 72 * (NB - 1), 0, base + 72)

    ramp = max(T_FAR, T_Y) + 2 + NSEND
    base = lax.fori_loop(0, ramp, functools.partial(step, full=True), jnp.int32(0))
    base = lax.fori_loop(ramp, STEPS - ramp, functools.partial(step, full=False), base)
    lax.fori_loop(STEPS - ramp, STEPS, functools.partial(step, full=True), base)
    for back in range(NSEND, 0, -1):
        for kind in range(3):
            n = jnp.int32(STEPS - back)
            when(sends(kind, n, True), lambda kind=kind, n=n: copy(kind, n).wait_send())

    @pl.loop(0, 8)
    def _(xp):
        for i in range(3):
            for j in range(3):
                cell = 3 * i + j
                blocks = [flux[cell, pl.ds(lax.rem(v + xp, NB) * 72 + xp, 8, stride=9), :] for v in range(NB)]
                blocks = turn_blocks(blocks, -1)
                lo = jnp.concatenate(blocks[:16], axis=0).T
                hi = jnp.concatenate(blocks[16:] + [zero] * 7, axis=0).T
                parts, olds = [], []
                for octant, half, x_abs, y_abs, rev in row_groups(xp, i, j):
                    for zh in range(2):
                        part = 4 * (octant % 2) + 2 * ((octant // 2) % 2) + zh
                        row = 16 * octant + 8 * half
                        val = (lo, hi)[zh][row:row + 8]
                        if rev:
                            val = jnp.take_along_axis(val, flip_rows, axis=0)
                        where = (part, x_abs, pl.ds(y_abs, 8, stride=3))
                        olds.append(acc[where + (slice(None),)] + val)
                        parts.append(where)
                for where, val in zip(parts, olds):
                    acc[where + (slice(None),)] = val

    @pl.loop(0, NX)
    def _(x):
        for yt in range(NY // 8):
            rows = pl.ds(8 * yt, 8)
            up_a = acc[4, x, rows, :] + acc[6, x, rows, :]
            up_b = acc[5, x, rows, :] + acc[7, x, rows, :]
            dn_a = jnp.take_along_axis(acc[0, x, rows, :] + acc[2, x, rows, :], mirror, axis=1)
            dn_b = jnp.take_along_axis(acc[1, x, rows, :] + acc[3, x, rows, :], mirror, axis=1)
            out_ref[x, rows, pl.ds(0, 128)] = up_a + jnp.where(tail, dn_b, dn_a)
            out_ref[x, rows, pl.ds(128, 72)] = (up_b + dn_a)[:, :72]


def solution(mesh):
    grid_spec = P(("g", "x"), "y", None)

    def column_sweep(source, sigma_t, cos_x, cos_y, cos_z, weights):
        smem = pl.BlockSpec(memory_space=pltpu.SMEM)
        vmem = pl.BlockSpec(memory_space=pltpu.VMEM)
        return pl.pallas_call(
            kernel,
            out_shape=jax.ShapeDtypeStruct((NX, NY, NZ), F32),
            in_specs=[smem] * 4 + [vmem] * 2,
            out_specs=vmem,
            scratch_shapes=[
                pltpu.VMEM((2, 4, NX, NY, 128), F32),
                pltpu.VMEM((2, 9, ROWS, 128), F32),
                pltpu.VMEM((9, ROWS, 128), F32),
                pltpu.VMEM((8, NX, NY, 128), F32),
                pltpu.VMEM((8, 128), jnp.int32),
                pltpu.VMEM((5, 8, 128), F32),
                pltpu.VMEM((5, 8 * pl.cdiv(STEPS, 8), 128), F32),
                pltpu.VMEM((5, 8, 128), F32),
                pltpu.VMEM((224, 128), F32),
                pltpu.VMEM((24, 8, 128), F32),
                pltpu.VMEM((12, 8, 128), F32),
                pltpu.VMEM((9, 8, 128), F32),
                pltpu.VMEM((8, 128), F32),
                pltpu.VMEM((8, 128), F32),
                pltpu.VMEM((NSEND, 24, 128), F32),
                pltpu.VMEM((2, RING, 24, 128), F32),
                pltpu.VMEM((NSEND, 8, 128), F32),
                pltpu.VMEM((RING, 8, 128), F32),
                pltpu.VMEM((4, 2, 8, 128), F32),
                pltpu.SemaphoreType.DMA((2, NSEND)),
                pltpu.SemaphoreType.DMA((2, RING)),
                pltpu.SemaphoreType.DMA((NSEND,)),
                pltpu.SemaphoreType.DMA((RING,)),
            ],
            compiler_params=pltpu.CompilerParams(
                collective_id=0, has_side_effects=True, vmem_limit_bytes=60 * 1024 * 1024),
        )(cos_x, cos_y, cos_z, weights, source, sigma_t)

    return jax.shard_map(column_sweep, mesh=mesh, in_specs=(grid_spec, grid_spec, P(), P(), P(), P()),
                         out_specs=grid_spec, check_vma=False)
```

time: 211 us -> 127 us (0.60)
  Pallas kernels: 209 us -> 123 us
    pallas_call x1, Pallas kernels: 209 us -> 123 us  [column_sweep(): pl.pallas_call(kernel, out_shape=jax.ShapeDtypeStruct((NX, NY, NZ), F32),...]
where the time goes in v2:
time: 127 us; the launch traced here: 126 us
  Pallas kernels  123 us (97%)
  local copies, waits for them, and re-layouts  2.36 us (2%)
    pallas_call x1, Pallas kernels, column_sweep(): pl.pallas_call(kernel, out_shape=jax.ShapeDtypeStruct((NX, NY, NZ), F32),...  123 us

profile of v2, /device:TPU:2, one launch (start us, length us, event | category | flops | bytes accessed | tf_op | source)
XLA Modules:
  0.0 125.7 jit_solution(3744031997987392657)
XLA Ops:
  0.0 123.3 %shard_map.64 = f32[24,48,200]{2,1,0:T(8,128)} custom-call(f32[10]{0:T(128)} %cx_ref.1, f32[10]{0:T(128)} %cy_ref.1, f32[10]{0:T(128)} %cz_ref.1, f32[10]{0:T(128)} %wt_ref.1, f32[24,48,200]{2,1,0:T(8,128)} %src_ref.1, f32[24,48,200]{2,1,0:T(8,128)} %sig_ref.1), custom_call_target="tpu_custom_call" | custom-call | tf_op jit(solution)/shard_map/pallas_call | solution.py:371
  123.3 2.4 %copy.8 = f32[24,48,200]{2,1,0:T(8,128)} copy(f32[24,48,200]{2,1,0:T(8,128)} %shard_map.64) | data formatting | bytes 1843200
